TPU v7x, 512 devices: a whole 4x8x8 slice. The times are simulated.
512 devices in a mesh: grp: 8 (over x, core), pq: 64 (over y, z).
Axes of the slice: x: 4, y: 8, z: 8, core: 2. Of those that a mesh axis runs over, the one named last changes fastest.
Arguments:
- pair_blocks: bfloat16 [16, 1152, 128, 128], P('grp', 'pq'), may hold values from -6 to 6
- block_list: int32 [16, 1152], P('grp', 'pq'), may hold values from 0 to 2047, as said below
- block_count: int32 [16, 64], P('grp', 'pq'), may hold values from 1 to 18, as said below
- coef: bfloat16 [4096, 512], P('pq', 'grp'), may hold values from -0.09375 to 0.09375
Outputs:
- transformed: float32 [32, 512, 512], P('grp', 'pq')
Inputs may be any that keep to these rules, and one draw needn't show every extreme that they name: `block_list`: within one row the ids are distinct, each in 0 to 2 * 32^2 - 1. `block_count`: in every row some device has exactly 18 live slots.
All inputs are finite; a program needn't handle non-finite values.
Results may differ from a plain program's by a relative error of at most 0.0042.
Values may be sent and summed in bfloat16 or wider, within the bound.
A program may use at most 64 MiB of HBM per device.

v0:
```python
import jax
import jax.numpy as jnp
from jax import lax
from jax.sharding import PartitionSpec as P

KL_PANEL = 2


def in_order(tiles, dim):
    tiles = jnp.moveaxis(tiles, 0, dim)
    dims = tiles.shape
    return tiles.reshape(*dims[:dim], dims[dim] * dims[dim + 1], *dims[dim + 2 :])


def sent_to_all(x, axis):
    length = lax.axis_size(axis)
    return lax.all_to_all(jnp.broadcast_to(x[None], (length, *x.shape)), axis, 0, 0, tiled=True)


def collect(x, axis, dim):
    return in_order(sent_to_all(x, axis), dim)


def partner(value, axis, distance):
    mask = 2**distance
    pairs = [(source, source ^ mask) for source in range(lax.axis_size(axis))]
    return lax.ppermute(value, axis, pairs)


def in_blocks(x, dim, length):
    before, after = (x.shape[:dim], x.shape[dim + 1 :])
    return jnp.moveaxis(x.reshape(*before, length, -1, *after), dim, 0)


def summed_on_arrival(x, axis, dim):
    length = lax.axis_size(axis)
    tiles = lax.all_to_all(in_blocks(x, dim, length), axis, 0, 0, tiled=True)
    return jnp.sum(tiles.astype(jnp.float32), axis=0)


def block_term(block, ident, coef_full, tile, nblk):
    per_kl = nblk * nblk
    which = ident // per_kl
    row_blk = ident // nblk % nblk
    col_blk = ident % nblk
    col_coef = lax.dynamic_slice_in_dim(coef_full, col_blk * tile, tile, 0)
    row_coef = lax.dynamic_slice_in_dim(coef_full, row_blk * tile, tile, 0)
    half = jnp.dot(block, col_coef, preferred_element_type=jnp.float32).astype(jnp.bfloat16)
    term = lax.dot_general(
        row_coef, half, (((0,), (0,)), ((), ())), preferred_element_type=jnp.float32
    )
    return (which, term)


def add_term(total, which, term):
    current = lax.dynamic_index_in_dim(total, which, 0, keepdims=False)
    return lax.dynamic_update_index_in_dim(total, current + term, which, 0)


def body(pair_blocks, block_list, block_count, coef):
    coef_rows = collect(coef, "pq", 0)
    coef_full = lax.all_gather(coef_rows, "grp", axis=1, tiled=True)
    panels = pair_blocks.shape[0]
    tile = pair_blocks.shape[2]
    nblk = coef_full.shape[0] // tile
    width = coef_full.shape[1]
    empty = jnp.zeros((KL_PANEL, width, width), jnp.float32)
    size_pq = lax.axis_size("pq")
    bit = size_pq.bit_length() - 2
    other_blocks, other_list, other_count = partner(
        (pair_blocks, block_list, block_count), "pq", bit
    )
    upper = lax.axis_index("pq") // (size_pq // 2) % 2
    stacked_blocks = jnp.stack([pair_blocks, other_blocks])
    stacked_list = jnp.stack([block_list, other_list])
    pieces = []
    for panel in range(panels):
        own_count = block_count[panel, 0]
        far_count = other_count[panel, 0]
        first_count = jnp.where(upper == 1, far_count, own_count)
        combined = own_count + far_count
        middle = (combined + 1) // 2
        lower_bound = jnp.where(upper == 1, middle, 0)
        upper_bound = jnp.where(upper == 1, combined, middle)

        def step(slot, total):
            source = jnp.where(slot < first_count, upper, 1 - upper)
            place = jnp.where(slot < first_count, slot, slot - first_count)
            block = stacked_blocks[source, panel, place]
            ident = stacked_list[source, panel, place]
            which, term = block_term(block, ident, coef_full, tile, nblk)
            return add_term(total, which, term)

        totals = lax.fori_loop(lower_bound, upper_bound, step, empty)
        pieces.append(totals)
    joined = jnp.concatenate(pieces, 0)
    return summed_on_arrival(joined.astype(jnp.bfloat16), "pq", 1)


def solution(mesh):
    in_specs = (P("grp", "pq", None, None), P("grp", "pq"), P("grp", "pq"), P("pq", "grp"))
    out_specs = P("grp", "pq", None)
    return jax.shard_map(body, mesh=mesh, in_specs=in_specs, out_specs=out_specs, check_vma=False)
```

profile of v0, /device:TPU:28, one launch (start us, length us, event | category | flops | bytes accessed | tf_op | source)
XLA Modules:
  0.0 344.9 jit_solution(13873950537614120583)
XLA Ops:
  8.3 34.9 %all_to_all.10 = bf16[64,2,2048]{2,1,0:T(2,128)(2,1)S(1)} all-to-all(bf16[64,2,2048]{2,1,0:T(2,128)(2,1)S(1)} %reshape.10), channel_id=1, replica_groups=mesh['grp'=8,'pq'=64] {'pq'}, dimensions={0} | all-to-all | bytes 1048576 | tf_op jit(solution)/shard_map/all_to_all | solution.py:17
  44.6 1.6 reshape.9
  46.2 4.0 %collective-permute-start.2 = (bf16[2,18,128,128]{3,2,1,0:T(8,128)(2,1)S(1)}, bf16[2,18,128,128]{3,2,1,0:T(8,128)(2,1)S(1)}, u32[]{:S(2)}, u32[]{:S(2)}) collective-permute-start(bf16[2,18,128,128]{3,2,1,0:T(8,128)(2,1)S(1)} %copy-done), channel_id=1, source_target_pairs={{0,32},{1,33},{2,34},{3,35},{4,36},{5,37},{6,38},{7,39},{8,40},{9,... | collective-permute-start | bytes 3538952 | tf_op jit(solution)/shard_map/ppermute | solution.py:27
  50.3 5.7 %collective-permute-start = (s32[2,1]{0,1:T(1,128)S(1)}, s32[2,1]{0,1:T(1,128)S(1)}, u32[]{:S(2)}, u32[]{:S(2)}) collective-permute-start(s32[2,1]{0,1:T(1,128)S(1)} %copy-done.1), channel_id=1, source_target_pairs={{0,32},{1,33},{2,34},{3,35},{4,36},{5,37},{6,38},{7,39},{8,40},{9,... | collective-permute-start | bytes 32 | tf_op jit(solution)/shard_map/ppermute | solution.py:27
  56.0 4.0 %collective-permute-start.1 = (s32[2,18]{1,0:T(2,128)S(1)}, s32[2,18]{1,0:T(2,128)S(1)}, u32[]{:S(2)}, u32[]{:S(2)}) collective-permute-start(s32[2,18]{1,0:T(2,128)S(1)} %copy-done.2), channel_id=1, source_target_pairs={{0,32},{1,33},{2,34},{3,35},{4,36},{5,37},{6,38},{7,39},{8,40},{9,... | collective-permute-start | bytes 440 | tf_op jit(solution)/shard_map/ppermute | solution.py:27
  60.6 42.5 %collective-permute-done = s32[2,1]{0,1:T(1,128)S(1)} collective-permute-done((s32[2,1]{0,1:T(1,128)S(1)}, s32[2,1]{0,1:T(1,128)S(1)}, u32[]{:S(2)}, u32[]{:S(2)}) %collective-permute-start) | collective-permute-done | bytes 40 | tf_op jit(solution)/shard_map/ppermute | solution.py:27
  108.5 1.7 pad_maximum_fusion
  110.2 6.5 %copy.18 = bf16[4096,512]{1,0:T(8,128)(2,1)} copy(bf16[4096,512]{0,1:T(8,128)(2,1)} %all-gather.2.cloned.1.call-done) | data formatting | bytes 8388608 | tf_op jit(solution)/shard_map/while | solution.py:94
  116.6 1.6 broadcast_in_dim.24.clone
  118.2 76.9 %while.27 = (s32[]{:T(128)}, f32[2,512,512]{2,1,0:T(8,128)}, s32[]{:T(128)}, s32[]{:T(128)}, s32[]{:T(128)}, /*index=5*/s32[]{:T(128)}, s32[2,2,18]{2,1,0:T(2,12...) while((s32[]{:T(128)}, f32[2,512,512]{2,1,0:T(8,128)}, ...), condition=%wide.region_3.4_spmd, body=%wide.region_2.3_spmd.sunk | while | flops 84213824 | bytes 4490093 | solution.py:94
  121.5 1.3 constant_dynamic-slice_fusion.11
  122.8 2.4 fusion.41
  128.5 1.3 constant_dynamic-slice_fusion.11
  129.8 2.4 fusion.41
  135.5 1.3 constant_dynamic-slice_fusion.11
  136.8 2.4 fusion.41
  142.5 1.3 constant_dynamic-slice_fusion.11
  143.8 2.4 fusion.41
  149.5 1.3 constant_dynamic-slice_fusion.11
  150.8 2.4 fusion.41
  156.5 1.3 constant_dynamic-slice_fusion.11
  157.8 2.4 fusion.41
  163.5 1.3 constant_dynamic-slice_fusion.11
  164.8 2.4 fusion.41
  170.5 1.3 constant_dynamic-slice_fusion.11
  171.8 2.4 fusion.41
  177.4 1.3 constant_dynamic-slice_fusion.11
  178.7 2.4 fusion.41
  184.4 1.3 constant_dynamic-slice_fusion.11
  185.7 2.4 fusion.41
  191.4 1.3 constant_dynamic-slice_fusion.11
  192.7 2.4 fusion.41
  195.4 53.6 %while.26 = (s32[]{:T(128)}, f32[2,512,512]{2,1,0:T(8,128)S(1)}, s32[]{:T(128)}, s32[]{:T(128)}, s32[]{:T(128)}, /*index=5*/s32[]{:T(128)}, s32[2,2,18]{2,1,0:T(...) while((s32[]{:T(128)}, f32[2,512,512]{2,1,0:T(8,128)S(1)}, ...), condition=%wide.region_1.2_spmd, body=%wide.region_0.1_spmd.sunk | while | flops 84213824 | bytes 4490093 | solution.py:94
  198.4 1.4 fusion.37
  202.9 1.4 fusion.37
  207.4 1.4 fusion.37
  211.8 1.4 fusion.37
  216.3 1.4 fusion.37
  220.8 1.4 fusion.37
  225.2 1.4 fusion.37
  229.7 1.4 fusion.37
  234.1 1.4 fusion.37
  238.6 1.4 fusion.37
  243.1 1.4 fusion.37
  247.5 1.4 fusion.37
  249.0 1.9 convert_bitcast_fusion
  251.3 85.8 %all_to_all.11 = bf16[64,4,8,512]{3,2,1,0:T(8,128)(2,1)S(1)} all-to-all(bf16[64,4,8,512]{3,2,1,0:T(8,128)(2,1)S(1)} %copy.20), channel_id=1, replica_groups=mesh['grp'=8,'pq'=64] {'pq'}, dimensions={0} | all-to-all | bytes 4194304 | tf_op jit(solution)/shard_map/all_to_all | solution.py:37
  337.1 1.0 convert_reduce_fusion
  (57 shorter events, 20.0 us)
Async XLA Ops:
  6.5 103.6 %all-gather.2.cloned.1.call-start = ((), (), s32[]{:S(2)}) async-start(), calls=%async_computation.2 | async-start | bytes 4718592 | tf_op jit(solution)/shard_map/all_gather | solution.py:62
  43.9 2.4 copy-start
  43.9 6.4 %copy-start.1 = (s32[2,1]{0,1:T(1,128)S(1)}, s32[2,1]{0,1:T(1,128)}, u32[]{:S(2)}) copy-start(s32[2,1]{0,1:T(1,128)} %param.10) | copy-start | bytes 28
  43.9 12.1 %copy-start.2 = (s32[2,18]{1,0:T(2,128)S(1)}, s32[2,18]{1,0:T(2,128)}, u32[]{:S(2)}) copy-start(s32[2,18]{1,0:T(2,128)} %param.9) | copy-start | bytes 436
  46.2 62.2 %collective-permute-start.2 = (bf16[2,18,128,128]{3,2,1,0:T(8,128)(2,1)S(1)}, bf16[2,18,128,128]{3,2,1,0:T(8,128)(2,1)S(1)}, u32[]{:S(2)}, u32[]{:S(2)}) collective-permute-start(bf16[2,18,128,128]{3,2,1,0:T(8,128)(2,1)S(1)} %copy-done), channel_id=1, source_target_pairs={{0,32},{1,33},{2,34},{3,35},{4,36},{5,37},{6,38},{7,39},{8,40},{9,... | collective-permute-start | bytes 3538952 | tf_op jit(solution)/shard_map/ppermute | solution.py:27
  50.3 52.9 %collective-permute-start = (s32[2,1]{0,1:T(1,128)S(1)}, s32[2,1]{0,1:T(1,128)S(1)}, u32[]{:S(2)}, u32[]{:S(2)}) collective-permute-start(s32[2,1]{0,1:T(1,128)S(1)} %copy-done.1), channel_id=1, source_target_pairs={{0,32},{1,33},{2,34},{3,35},{4,36},{5,37},{6,38},{7,39},{8,40},{9,... | collective-permute-start | bytes 32 | tf_op jit(solution)/shard_map/ppermute | solution.py:27
  56.0 52.4 %collective-permute-start.1 = (s32[2,18]{1,0:T(2,128)S(1)}, s32[2,18]{1,0:T(2,128)S(1)}, u32[]{:S(2)}, u32[]{:S(2)}) collective-permute-start(s32[2,18]{1,0:T(2,128)S(1)} %copy-done.2), channel_id=1, source_target_pairs={{0,32},{1,33},{2,34},{3,35},{4,36},{5,37},{6,38},{7,39},{8,40},{9,... | collective-permute-start | bytes 440 | tf_op jit(solution)/shard_map/ppermute | solution.py:27
Sparse Core Ops, SparseCore 0:
  46.4 29.9 all-gather.1
where the time goes:
time: 343 us; the launch traced here: 345 us
  blocking collectives  121 us (35%)
  loops' own time  57.2 us (17%)
  matrix products  44 us (13%)
  local copies, waits for them, and re-layouts  43.7 us (13%)
  waiting for transfers between devices  42.5 us (12%)
  between operations  18.3 us (5%)
  starting transfers between devices  13.8 us (4%)
  other arithmetic  4.69 us (1%)
    all_to_all x1, blocking collectives, summed_on_arrival(): tiles = lax.all_to_all(in_blocks(x, dim, length), axis, 0, 0, tiled=True)  85.8 us
    another operation x2, loops' own time, body(): totals = lax.fori_loop(lower_bound, upper_bound, step, empty)  57.2 us
    dot_general x23, matrix products, block_term(): lax.dot_general(row_coef, half, (((0,), (0,)), ((), ())), preferred_eleme...  44 us
    ppermute x3, waiting for transfers between devices, partner(): return lax.ppermute(value, axis, pairs)  42.5 us
    all_to_all x1, blocking collectives, sent_to_all(): lax.all_to_all(jnp.broadcast_to(x[None], (length, *x.shape)), axis, 0, 0,...  34.9 us
    dynamic_slice x23, local copies, waits for them, and re-layouts, add_term(): current = lax.dynamic_index_in_dim(total, which, 0, keepdims=False)  15.2 us
    dynamic_slice x23, local copies, waits for them, and re-layouts, step(): ident = stacked_list[source, panel, place]  14.1 us
    ppermute x3, starting transfers between devices, partner(): return lax.ppermute(value, axis, pairs)  13.8 us
  transfers between devices with their start and end apart: 4, of which 1 were waited for; matrix products, arithmetic and copies ran while one was open for 1% of the time, Pallas kernels for 0%

commit v1 on v0

v1 whole, which is shorter than its diff:
```python
import jax
import jax.numpy as jnp
from jax import lax
from jax.experimental import pallas as pl
from jax.experimental.pallas import tpu as pltpu
from jax.sharding import PartitionSpec as P

MESH = pl.DeviceIdType.MESH
SIDE = 8
HALF = SIDE // 2
TILE = 128
KL = 2
PLACE = (0, 1, 3, 5, 7, 6, 4, 2)


def remote(src, dst, send, recv, device):
    return pltpu.make_async_remote_copy(
        src_ref=src, dst_ref=dst, send_sem=send, recv_sem=recv, device_id=device, device_id_type=MESH
    )


def gather_kernel(coef_ref, out_ref, mine, raw, g_send, g_recv, a_send, a_recv, b_send, b_recv, d_send, d_recv):
    g, p = lax.axis_index("grp"), lax.axis_index("pq")
    core = g % 2
    y, z = p // SIDE, p % SIDE
    a = y * (1 - core) + z * core
    b = z * (1 - core) + y * core
    step_a = SIDE * (1 - core) + core
    step_b = (1 - core) + SIDE * core

    def at(a_to, b_to):
        return (g, a_to * step_a + b_to * step_b)

    grp_peers = [((g + j) % 8, p) for j in range(1, 8)]
    a_peers = [at((a + d) % SIDE, b) for d in (1, 7, 2, 6, 3, 5, 4)]
    right, left = at(a, (b + 1) % SIDE), at(a, (b + 7) % SIDE)
    partner = (g + 1 - 2 * core, p)

    barrier = pltpu.get_barrier_semaphore()
    peers = grp_peers + a_peers + [right, left]
    for device in peers:
        pl.semaphore_signal(barrier, inc=1, device_id=device, device_id_type=MESH)
    mine[...] = jnp.concatenate([coef_ref[...], coef_ref[...]], axis=1)
    raw[g] = mine[pl.ds(pl.multiple_of(core * 32, 32), 32), :]
    pl.semaphore_wait(barrier, len(peers))

    sent = []
    for j in range(1, 8):
        g_to = (g + j) % 8
        rows = pl.ds(pl.multiple_of((g_to % 2) * 32, 32), 32)
        copy = remote(mine.at[rows, :], raw.at[g], g_send.at[j], g_recv.at[j], (g_to, p))
        copy.start()
        sent.append(copy)
    for copy in sent:
        copy.wait_recv()
    low = lax.broadcasted_iota(jnp.int32, (32, TILE), 1) < TILE // 2
    for x in range(4):
        out_ref[core, b, 0, x] = jnp.where(low, raw[2 * x], raw[2 * x + 1])

    arrivals = {}
    for n, d in enumerate((1, 7, 2, 6, 3, 5, 4)):
        place = PLACE[(8 - d) % 8]
        copy = remote(out_ref.at[core, b, 0], out_ref.at[core, b, place], a_send.at[place], a_recv.at[place], a_peers[n])
        copy.start()
        sent.append(copy)
        arrivals[place] = copy

    def line(b_from, part):
        return out_ref.at[core, b_from, pl.ds(HALF * part, HALF)]

    def pass_on(way, part, step, b_from):
        block = line(b_from, part)
        hops = HALF if way == part else HALF - 1
        if step < hops:
            copy = remote(block, block, b_send.at[way, part, step], b_recv.at[way, part, step], (right, left)[way])
            copy.start()
            sent.append(copy)
            flights[way, part, step + 1] = copy
        if step > 0 or way == 0:
            n = (way * 2 + part) * (HALF + 1) + step
            copy = remote(block, block, d_send.at[n], d_recv.at[n], partner)
            copy.start()
            sent.append(copy)
            across.append(copy)

    flights, across = {}, []
    for part in range(2):
        for place in range(HALF * part, HALF * part + HALF):
            if place > 0:
                arrivals[place].wait_recv()
        for way in range(2):
            pass_on(way, part, 0, b)
    for step in range(1, HALF + 1):
        for part in range(2):
            for way in range(2):
                if (way, part, step) in flights:
                    flights[way, part, step].wait_recv()
                    away = step if way == 0 else 8 - step
                    pass_on(way, part, step, (b + 8 - away) % SIDE)
    for copy in across:
        copy.wait_recv()
    for copy in sent:
        copy.wait_send()


def gather(coef):
    return pl.pallas_call(
        gather_kernel,
        name="gather_coef",
        out_shape=jax.ShapeDtypeStruct((2, SIDE, SIDE, 4, 32, TILE), jnp.bfloat16),
        in_specs=[pl.BlockSpec(memory_space=pltpu.VMEM)],
        out_specs=pl.BlockSpec(memory_space=pltpu.VMEM),
        scratch_shapes=[
            pltpu.VMEM((64, TILE), jnp.bfloat16),
            pltpu.VMEM((8, 32, TILE), jnp.bfloat16),
            pltpu.SemaphoreType.DMA((8,)),
            pltpu.SemaphoreType.DMA((8,)),
            pltpu.SemaphoreType.DMA((8,)),
            pltpu.SemaphoreType.DMA((8,)),
            pltpu.SemaphoreType.DMA((2, 2, 4)),
            pltpu.SemaphoreType.DMA((2, 2, 4)),
            pltpu.SemaphoreType.DMA((20,)),
            pltpu.SemaphoreType.DMA((20,)),
        ],
        compiler_params=pltpu.CompilerParams(collective_id=0, has_side_effects=True),
    )(coef)


def transform_kernel(list_ref, count_ref, blocks_ref, coef_ref, out_ref, half_ref, left_ref):
    p = lax.axis_index("pq")
    y_me, z_me = p // SIDE, p % SIDE
    slots = blocks_ref.shape[1]
    nblk = SIDE * SIDE // 2

    def place(k):
        k = (k + SIDE) % SIDE
        return jnp.where(k == 0, 0, jnp.where(k <= HALF, 2 * k - 1, 16 - 2 * k))

    def rows_of(tile):
        parts = []
        for e in range(2):
            y, z = tile // 4, 2 * (tile % 4) + e
            parts.append(coef_ref[0, z, place(y - y_me)])
            parts.append(coef_ref[1, y, place(z - z_me)])
        return [jnp.concatenate([part[x] for part in parts], axis=0) for x in range(4)]

    for panel in range(2):

        def one_slot(slot, carry):
            ident = list_ref[panel, slot]
            live = slot < count_ref[panel, 0]
            which = ident // (nblk * nblk)
            at = pl.ds(pl.multiple_of(slot * TILE, TILE), TILE)
            cols = jnp.concatenate(rows_of(ident % nblk), axis=1)
            half = jnp.dot(blocks_ref[panel, slot], cols, preferred_element_type=jnp.float32)
            half_ref[at, :] = half.astype(jnp.bfloat16)
            rows = rows_of(ident // nblk % nblk)
            keep = [(live & (which == kl)).astype(jnp.float32) for kl in range(KL)]
            for x in range(4):
                turned = rows[x].astype(jnp.float32).T
                for kl in range(KL):
                    left_ref[x, pl.ds(kl * TILE, TILE), at] = (turned * keep[kl]).astype(jnp.bfloat16)
            return carry

        lax.fori_loop(0, slots, one_slot, 0)
        for x in range(4):
            sums = jnp.dot(left_ref[x], half_ref[...], preferred_element_type=jnp.float32)
            groups = sums.reshape(KL, 2, SIDE, 8, sums.shape[1])
            both = jnp.concatenate([groups[0], groups[1]], axis=2).astype(jnp.bfloat16)
            for n in range(2):
                if panel == 0:
                    out_ref[0, 2 * x + n] = both[n]
                else:
                    for zz in range(SIDE):
                        out_ref[1, zz, 2 * x + n] = both[n, zz]


def transform(block_list, block_count, pair_blocks, coef_all):
    panels, slots = pair_blocks.shape[:2]
    nmo = 4 * TILE
    return pl.pallas_call(
        transform_kernel,
        name="transform_blocks",
        out_shape=jax.ShapeDtypeStruct((panels, SIDE, SIDE, KL * 8, nmo), jnp.bfloat16),
        in_specs=[
            pl.BlockSpec(memory_space=pltpu.SMEM),
            pl.BlockSpec(memory_space=pltpu.SMEM),
            pl.BlockSpec(memory_space=pltpu.VMEM),
            pl.BlockSpec(memory_space=pltpu.VMEM),
        ],
        out_specs=pl.BlockSpec(memory_space=pltpu.VMEM),
        scratch_shapes=[
            pltpu.VMEM((slots * TILE, nmo), jnp.bfloat16),
            pltpu.VMEM((4, KL * TILE, slots * TILE), jnp.bfloat16),
        ],
    )(block_list, block_count, pair_blocks, coef_all)


def scatter_kernel(part_ref, out_ref, came, total, final, r_send, r_recv, b_send, b_recv):
    g, p = lax.axis_index("grp"), lax.axis_index("pq")
    y, z = p // SIDE, p % SIDE
    first, second = (y, z), (z, y)
    steps = ((SIDE, 1), (1, SIDE))

    def at(panel, a_to, b_to):
        return (g, a_to * steps[panel][0] + b_to * steps[panel][1])

    barrier = pltpu.get_barrier_semaphore()
    peers = [at(panel, first[panel], (second[panel] + d) % SIDE) for panel in range(2) for d in range(1, 8)]
    for device in peers:
        pl.semaphore_signal(barrier, inc=1, device_id=device, device_id_type=MESH)
    pl.semaphore_wait(barrier, len(peers))

    sent, flights = [], {}

    def hop(panel, way, part, step):
        a = first[panel]
        hops = HALF if way == part else HALF - 1
        away = hops - step
        dest = (a + (away if way == 0 else 8 - away)) % SIDE
        rows = pl.ds(HALF * part, HALF)
        n = ((panel * 2 + way) * 2 + part) * HALF + step
        own = part_ref.at[panel, dest, rows]
        if step > 0:
            held = came.at[n - 1]
            held[...] = (own[...].astype(jnp.float32) + held[...].astype(jnp.float32)).astype(jnp.bfloat16)
        else:
            held = own
        neighbour = at(panel, (a + (1 if way == 0 else 7)) % SIDE, second[panel])
        copy = remote(held, came.at[n], r_send.at[n], r_recv.at[n], neighbour)
        copy.start()
        sent.append(copy)
        flights[panel, way, part, step] = copy

    order = [(panel, way, part) for part in range(2) for panel in range(2) for way in range(2)]
    for panel, way, part in order:
        hop(panel, way, part, 0)
    for step in range(1, HALF + 1):
        for panel, way, part in order:
            hops = HALF if way == part else HALF - 1
            if step <= hops:
                flights[panel, way, part, step - 1].wait_recv()
            if step < hops:
                hop(panel, way, part, step)
    for panel in range(2):
        for part in range(2):
            rows = pl.ds(HALF * part, HALF)
            whole = part_ref[panel, first[panel], rows].astype(jnp.float32)
            for way in range(2):
                hops = HALF if way == part else HALF - 1
                n = ((panel * 2 + way) * 2 + part) * HALF + hops - 1
                whole = whole + came[n].astype(jnp.float32)
            total[panel, rows] = whole.astype(jnp.bfloat16)
    straight = []
    for panel in range(2):
        for d in (4, 3, 5, 2, 6, 1, 7):
            b_to = (second[panel] + d) % SIDE
            n = panel * SIDE + d
            copy = remote(total.at[panel, b_to], final.at[n], b_send.at[n], b_recv.at[n], at(panel, first[panel], b_to))
            copy.start()
            sent.append(copy)
            straight.append(copy)
    for copy in straight:
        copy.wait_recv()
    for panel in range(2):
        rows = total[panel, second[panel]].astype(jnp.float32)
        for d in range(1, 8):
            rows = rows + final[panel * SIDE + d].astype(jnp.float32)
        out_ref[KL * panel] = rows[:8]
        out_ref[KL * panel + 1] = rows[8:]
    for copy in sent:
        copy.wait_send()


def scatter(parts):
    panels, nmo = parts.shape[0], parts.shape[-1]
    return pl.pallas_call(
        scatter_kernel,
        name="reduce_scatter",
        out_shape=jax.ShapeDtypeStruct((panels * KL, 8, nmo), jnp.float32),
        in_specs=[pl.BlockSpec(memory_space=pltpu.VMEM)],
        out_specs=pl.BlockSpec(memory_space=pltpu.VMEM),
        scratch_shapes=[
            pltpu.VMEM((32, HALF, 16, nmo), jnp.bfloat16),
            pltpu.VMEM((2, SIDE, 16, nmo), jnp.bfloat16),
            pltpu.VMEM((2 * SIDE, 16, nmo), jnp.bfloat16),
            pltpu.SemaphoreType.DMA((32,)),
            pltpu.SemaphoreType.DMA((32,)),
            pltpu.SemaphoreType.DMA((16,)),
            pltpu.SemaphoreType.DMA((16,)),
        ],
        compiler_params=pltpu.CompilerParams(collective_id=1, has_side_effects=True),
    )(parts)


def body(pair_blocks, block_list, block_count, coef):
    coef_all = gather(coef)
    parts = transform(block_list, block_count, pair_blocks, coef_all)
    return scatter(parts)


def solution(mesh):
    in_specs = (P("grp", "pq", None, None), P("grp", "pq"), P("grp", "pq"), P("pq", "grp"))
    out_specs = P("grp", "pq", None)
    return jax.shard_map(body, mesh=mesh, in_specs=in_specs, out_specs=out_specs, check_vma=False)
```

time: 343 us -> 97 us (0.28)
  the two profiles are of different devices: /device:TPU:28 before, /device:TPU:8 now
where the time goes in v1:
time: 97 us; the launch traced here: 96.7 us
  Pallas kernels  93.9 us (97%)
  local copies, waits for them, and re-layouts  2.77 us (3%)
    pallas_call x1, Pallas kernels, gather(): pl.pallas_call(gather_kernel, name='gather_coef', out_shape=jax.ShapeDtyp...  44.1 us
    pallas_call x1, Pallas kernels, scatter(): pl.pallas_call(scatter_kernel, name='reduce_scatter', out_shape=jax.Shape...  33.4 us
    pallas_call x1, Pallas kernels, transform(): pl.pallas_call(transform_kernel, name='transform_blocks', out_shape=jax.S...  16.4 us
    unnamed x2, local copies, waits for them, and re-layouts  2.77 us

profile of v1, /device:TPU:8, one launch (start us, length us, event | category | flops | bytes accessed | tf_op | source)
XLA Modules:
  0.0 96.7 jit_solution(4976235708993415322)
XLA Ops:
  0.0 1.3 %copy.5.count_ref = s32[2,1]{1,0:T(2,128)} copy(s32[2,1]{0,1:T(1,128)} %param.6) | data formatting | bytes 16 | tf_op args[2]
  1.3 44.1 %gather_coef.1.coef_ref = bf16[2,8,8,4,32,128]{5,4,3,2,1,0:T(8,128)(2,1)} custom-call(bf16[64,64]{1,0:T(8,128)(2,1)} %coef_ref.1), custom_call_target="tpu_custom_call" | custom-call | tf_op jit(solution)/shard_map/gather_coef/pallas_call | solution.py:107
  45.4 16.4 %transform_blocks.1.part_ref = bf16[2,8,8,16,512]{4,3,2,1,0:T(8,128)(2,1)} custom-call(s32[2,18]{1,0:T(2,128)} %list_ref.1, s32[2,1]{1,0:T(2,128)} %copy.5.count_ref, bf16[2,18,128,128]{3,2,1,0:T(8,128)(2,1)} %blocks_ref.1, bf16[2,8,8,4,32,128]{5,4,3,2,1,0:T(8,128)(2,1)} %gather_coef.1.coef_ref), custom_call_target="tpu_custom_call" | custom-call | tf_op jit(solution)/shard_map/transform_blocks/pallas_call | solution.py:181
  61.8 33.4 %reduce_scatter.1 = f32[4,8,512]{2,1,0:T(8,128)} custom-call(bf16[2,8,8,16,512]{4,3,2,1,0:T(8,128)(2,1)} %transform_blocks.1.part_ref), custom_call_target="tpu_custom_call" | custom-call | tf_op jit(solution)/shard_map/reduce_scatter/pallas_call | solution.py:277
  95.2 1.5 %copy.7 = f32[4,8,512]{2,1,0:T(8,128)} copy(f32[4,8,512]{2,1,0:T(8,128)} %reduce_scatter.1) | data formatting | bytes 131072

commit v2 on v0

v2 whole, which is shorter than its diff:
```python
import jax
import jax.numpy as jnp
from jax import lax
from jax.experimental import pallas as pl
from jax.experimental.pallas import tpu as pltpu
from jax.sharding import PartitionSpec as P

MESH = pl.DeviceIdType.MESH
SIDE = 8
FAR = SIDE // 2
TILE = 128
KL = 2
BF16 = jnp.bfloat16
NEAR_FIRST = (0, 1, 7, 2, 6, 3, 5, 4)
FAR_FIRST = (4, 3, 5, 2, 6, 1, 7, 0)
PARTS = 4
ROWS = SIDE // PARTS


def near_place(k):
    n = (k + 2 * SIDE - 1) % SIDE
    return 2 * n + 1 + (n // FAR) * (13 - 4 * n)


def far_place(k):
    m = (k + SIDE + FAR) % SIDE
    return 2 * m + (m // FAR) * (15 - 4 * m)


def hops_of(way, part):
    return FAR - (way + part) % 2


def remote(src, dst, send, recv, device):
    return pltpu.make_async_remote_copy(
        src_ref=src, dst_ref=dst, send_sem=send, recv_sem=recv, device_id=device, device_id_type=MESH
    )


def kernel(
    list_ref, count_ref, blocks_hbm, coef_hbm, out_ref,
    own, mine, raw, coef, blocks, half, left, sums, came, total, final,
    in_sem, g_send, g_recv, a_send, a_recv, b_send, b_recv, d_send, d_recv, r_send, r_recv, s_send, s_recv,
):
    g, p = lax.axis_index("grp"), lax.axis_index("pq")
    core = g % 2
    y, z = p // SIDE, p % SIDE
    slots = blocks.shape[1]
    nblk = SIDE * FAR

    barrier = pltpu.get_barrier_semaphore()
    peers = [((g + j) % 8, p) for j in range(1, 8)]
    peers += [(g, (y + d) % SIDE * SIDE + z) for d in range(1, 8)]
    peers += [(g, y * SIDE + (z + d) % SIDE) for d in range(1, 8)]
    for device in peers:
        pl.semaphore_signal(barrier, inc=1, device_id=device, device_id_type=MESH)
    load_coef = pltpu.make_async_copy(coef_hbm, own, in_sem.at[0])
    load_blocks = pltpu.make_async_copy(blocks_hbm, blocks, in_sem.at[1])
    load_coef.start()
    load_blocks.start()
    load_coef.wait()
    mine[...] = jnp.concatenate([own[...], own[...]], axis=1)
    raw[g] = mine[pl.ds(pl.multiple_of(core * 32, 32), 32), :]
    pl.semaphore_wait(barrier, len(peers))

    a = y * (1 - core) + z * core
    b = z * (1 - core) + y * core
    step_a = SIDE * (1 - core) + core
    step_b = (1 - core) + SIDE * core
    partner = (g + 1 - 2 * core, p)
    beside = [(g, a * step_a + (b + 1) % SIDE * step_b), (g, a * step_a + (b + 7) % SIDE * step_b)]

    for j in range(1, 8):
        g_to = (g + j) % 8
        rows = pl.ds(pl.multiple_of((g_to % 2) * 32, 32), 32)
        remote(mine.at[rows, :], raw.at[g], g_send, g_recv, (g_to, p)).start()
    seven = raw.at[pl.ds(0, 7)]
    remote(seven, seven, g_send, g_recv, partner).wait_recv()
    low = lax.broadcasted_iota(jnp.int32, (32, TILE), 1) < TILE // 2
    for x in range(4):
        coef[core, b, 0, x] = jnp.where(low, raw[2 * x], raw[2 * x + 1])

    straight = {}
    for d in NEAR_FIRST[1:]:
        place = NEAR_FIRST.index(SIDE - d)
        to = (g, (a + d) % SIDE * step_a + b * step_b)
        straight[place] = remote(coef.at[core, b, 0], coef.at[core, b, place], a_send, a_recv.at[place], to)
        straight[place].start()

    flights, held = {}, {}

    def send_on(way, place, step):
        away = step if way == 1 else SIDE - step
        b_from = (b + away) % SIDE
        if step < hops_of(way, place):
            piece = coef.at[core, b_from, place]
            copy = remote(piece, piece, b_send, b_recv.at[way, place, step], beside[way])
            copy.start()
            flights[way, place, step + 1] = copy
        if step > 0 or way == 0:
            pair = held.setdefault((away % SIDE, place // 2), set())
            pair.add(place)
            if len(pair) == 2:
                piece = coef.at[core, b_from, pl.ds(place // 2 * 2, 2)]
                remote(piece, piece, d_send, d_recv, partner).start()

    ready = (0.0, 2.2, 2.2, 3.2, 3.2, 4.4, 4.4, 5.6)
    events = sorted(
        (ready[place] + 0.35 * place + 2.6 * step, place, way, step)
        for place in range(SIDE)
        for way in range(2)
        for step in range(hops_of(way, place) + 1)
    )
    for _, place, way, step in events:
        if step > 0:
            flights[way, place, step].wait_recv()
        elif place > 0 and way == 0:
            straight[place].wait_recv()
        send_on(way, place, step)
    remote(coef.at[0], coef.at[0], d_send, d_recv, partner).wait_recv()
    load_blocks.wait()

    def rows_of(tile):
        pieces = []
        for e in range(2):
            y_of, z_of = tile // 4, 2 * (tile % 4) + e
            pieces.append(coef[0, z_of, near_place(y_of - y)])
            pieces.append(coef[1, y_of, near_place(z_of - z)])
        return [jnp.concatenate([piece[x] for piece in pieces], axis=0) for x in range(4)]

    def transform(panel):
        def one_slot(slot, carry):
            ident = list_ref[panel, slot]
            live = slot < count_ref[0, panel]
            which = ident // (nblk * nblk)
            at = pl.ds(pl.multiple_of(slot * TILE, TILE), TILE)
            cols = jnp.concatenate(rows_of(ident % nblk), axis=1)
            half[at, :] = jnp.dot(blocks[panel, slot], cols, preferred_element_type=jnp.float32).astype(BF16)
            rows = rows_of(ident // nblk % nblk)
            keep = [(live & (which == kl)).astype(jnp.float32).astype(BF16) for kl in range(KL)]
            for x in range(4):
                turned = rows[x].T
                for kl in range(KL):
                    left[x, pl.ds(kl * TILE, TILE), at] = turned * keep[kl]
            return carry

        lax.fori_loop(0, slots, one_slot, 0, unroll=3)
        for x in range(4):
            block = jnp.dot(left[x], half[...], preferred_element_type=jnp.float32)
            block = block.reshape(KL, 2, SIDE, 8, block.shape[1])
            block = jnp.concatenate([block[0], block[1]], axis=2).astype(BF16)
            for n in range(2):
                for i in range(SIDE):
                    if panel == 0:
                        sums[0, 2 * x + n, far_place(i - z)] = block[n, i]
                    else:
                        sums[1, i, far_place(2 * x + n - y)] = block[n, i]

    first, second = (y, z), (z, y)
    steps = ((SIDE, 1), (1, SIDE))
    numbers = {}
    for panel in range(2):
        for part in range(PARTS):
            for way in range(2):
                for step in range(hops_of(way, part)):
                    numbers[panel, way, part, step] = len(numbers)
    hopping = {}

    def hop(panel, way, part, step):
        away = hops_of(way, part) - step
        dest = (first[panel] + (away if way == 0 else SIDE - away)) % SIDE
        rows = pl.ds(ROWS * part, ROWS)
        piece = sums.at[panel, dest, rows]
        if step > 0:
            sofar = came.at[numbers[panel, way, part, step - 1]]
            sofar[...] = (piece[...].astype(jnp.float32) + sofar[...].astype(jnp.float32)).astype(BF16)
            piece = sofar
        n = numbers[panel, way, part, step]
        a_to = (first[panel] + (1 if way == 0 else 7)) % SIDE
        to = (g, a_to * steps[panel][0] + second[panel] * steps[panel][1])
        copy = remote(piece, came.at[n], r_send, r_recv.at[n], to)
        copy.start()
        hopping[panel, way, part, step + 1] = copy

    def finish(panel, part):
        rows = pl.ds(ROWS * part, ROWS)
        whole = sums[panel, first[panel], rows].astype(jnp.float32)
        for way in range(2):
            whole = whole + came[numbers[panel, way, part, hops_of(way, part) - 1]].astype(jnp.float32)
        total[panel, rows] = whole.astype(BF16)
        for i in range(ROWS * part, ROWS * part + ROWS):
            d = FAR_FIRST[i]
            if d:
                to = (g, first[panel] * steps[panel][0] + (second[panel] + d) % SIDE * steps[panel][1])
                copy = remote(total.at[panel, i], final.at[panel, i], s_send, s_recv.at[panel], to)
                copy.start()

    for panel in range(2):
        transform(panel)
        for part in range(PARTS):
            for way in range(2):
                hop(panel, way, part, 0)
    for step in range(1, FAR + 1):
        for part in range(PARTS):
            for panel in range(2):
                for way in range(2):
                    if step <= hops_of(way, part):
                        hopping[panel, way, part, step].wait_recv()
                    if step < hops_of(way, part):
                        hop(panel, way, part, step)
                if step == FAR:
                    finish(panel, part)
    for panel in range(2):
        seven = final.at[panel, pl.ds(0, 7)]
        remote(seven, seven, s_send, s_recv.at[panel], partner).wait_recv()
        rows = total[panel, SIDE - 1].astype(jnp.float32)
        for i in range(SIDE - 1):
            rows = rows + final[panel, i].astype(jnp.float32)
        out_ref[KL * panel] = rows[:8]
        out_ref[KL * panel + 1] = rows[8:]

    seven = raw.at[pl.ds(0, 7)]
    remote(seven, seven, g_send, g_recv, partner).wait_send()
    seven = coef.at[0, 0, pl.ds(0, 7)]
    remote(seven, seven, a_send, g_recv, partner).wait_send()
    seven = coef.at[0, pl.ds(0, 7)]
    remote(seven, seven, b_send, g_recv, partner).wait_send()
    remote(coef.at[0], coef.at[0], d_send, d_recv, partner).wait_send()
    remote(came, came, r_send, g_recv, partner).wait_send()
    for panel in range(2):
        seven = final.at[panel, pl.ds(0, 7)]
        remote(seven, seven, s_send, g_recv, partner).wait_send()


def body(pair_blocks, block_list, block_count, coef):
    panels, slots = pair_blocks.shape[:2]
    nmo = 4 * TILE
    dma = pltpu.SemaphoreType.DMA
    return pl.pallas_call(
        kernel,
        name="transform",
        out_shape=jax.ShapeDtypeStruct((panels * KL, 8, nmo), jnp.float32),
        in_specs=[
            pl.BlockSpec(memory_space=pltpu.SMEM),
            pl.BlockSpec(memory_space=pltpu.SMEM),
            pl.BlockSpec(memory_space=pl.ANY),
            pl.BlockSpec(memory_space=pl.ANY),
        ],
        out_specs=pl.BlockSpec(memory_space=pltpu.VMEM),
        scratch_shapes=[
            pltpu.VMEM(coef.shape, BF16),
            pltpu.VMEM((64, TILE), BF16),
            pltpu.VMEM((8, 32, TILE), BF16),
            pltpu.VMEM((2, SIDE, SIDE, 4, 32, TILE), BF16),
            pltpu.VMEM(pair_blocks.shape, BF16),
            pltpu.VMEM((slots * TILE, nmo), BF16),
            pltpu.VMEM((4, KL * TILE, slots * TILE), BF16),
            pltpu.VMEM((panels, SIDE, SIDE, KL * 8, nmo), BF16),
            pltpu.VMEM((2 * PARTS * 7, ROWS, KL * 8, nmo), BF16),
            pltpu.VMEM((panels, SIDE, KL * 8, nmo), BF16),
            pltpu.VMEM((panels, SIDE, KL * 8, nmo), BF16),
            dma((2,)),
            dma,
            dma,
            dma,
            dma((SIDE,)),
            dma,
            dma((2, SIDE, FAR)),
            dma,
            dma,
            dma,
            dma((2 * PARTS * 7,)),
            dma,
            dma((2,)),
        ],
        compiler_params=pltpu.CompilerParams(collective_id=0, has_side_effects=True),
    )(block_list, block_count.reshape(1, panels), pair_blocks, coef)


def solution(mesh):
    in_specs = (P("grp", "pq", None, None), P("grp", "pq"), P("grp", "pq"), P("pq", "grp"))
    out_specs = P("grp", "pq", None)
    return jax.shard_map(body, mesh=mesh, in_specs=in_specs, out_specs=out_specs, check_vma=False)
```

time: 343 us -> 75.8 us (0.22)
  the two profiles are of different devices: /device:TPU:28 before, /device:TPU:1 now
where the time goes in v2:
time: 75.8 us; the launch traced here: 75.6 us
  Pallas kernels  74.1 us (98%)
  local copies, waits for them, and re-layouts  1.47 us (2%)
    pallas_call x1, Pallas kernels, body(): pl.pallas_call(kernel, name='transform', out_shape=jax.ShapeDtypeStruct((...  74.1 us

profile of v2, /device:TPU:1, one launch (start us, length us, event | category | flops | bytes accessed | tf_op | source)
XLA Modules:
  0.0 75.6 jit_solution(908162584822836755)
XLA Ops:
  0.0 74.1 %transform.1 = f32[4,8,512]{2,1,0:T(8,128)} custom-call(s32[2,18]{1,0:T(2,128)} %list_ref.1, s32[1,2]{1,0:T(1,128)} %bitcast.1, bf16[2,18,128,128]{3,2,1,0:T(8,128)(2,1)} %blocks_hbm.1, bf16[64,64]{1,0:T(8,128)(2,1)} %coef_hbm.1), custom_call_target="tpu_custom_call" | custom-call | tf_op jit(solution)/shard_map/transform/pallas_call | solution.py:239
  74.1 1.5 %copy.6 = f32[4,8,512]{2,1,0:T(8,128)} copy(f32[4,8,512]{2,1,0:T(8,128)} %transform.1) | data formatting | bytes 131072

commit v3 on v2

v3 whole, which is shorter than its diff:
```python
import jax
import jax.numpy as jnp
from jax import lax
from jax.experimental import pallas as pl
from jax.experimental.pallas import tpu as pltpu
from jax.sharding import PartitionSpec as P

MESH = pl.DeviceIdType.MESH
SIDE = 8
FAR = SIDE // 2
TILE = 128
KL = 2
BF16 = jnp.bfloat16
NEAR_FIRST = (0, 1, 7, 2, 6, 3, 5, 4)
FAR_FIRST = (4, 3, 5, 2, 6, 1, 7, 0)
PARTS = 4
ROWS = SIDE // PARTS
UNROLL = 6


def near_place(k):
    n = (k + 2 * SIDE - 1) % SIDE
    return 2 * n + 1 + (n // FAR) * (13 - 4 * n)


def far_place(k):
    m = (k + SIDE + FAR) % SIDE
    return 2 * m + (m // FAR) * (15 - 4 * m)


def hops_of(way, part):
    return FAR - (way + part) % 2


def remote(src, dst, send, recv, device):
    return pltpu.make_async_remote_copy(
        src_ref=src, dst_ref=dst, send_sem=send, recv_sem=recv, device_id=device, device_id_type=MESH
    )


def kernel(
    list_ref, count_ref, blocks_hbm, coef_hbm, out_ref,
    own, mine, theirs, coef, blocks, half, left, sums, came, total, final,
    in_sem, o_send, o_recv, x_send, x_recv, a_send, a_recv, b_send, b_recv, d_send, d_recv, r_send, r_recv, s_send, s_recv,
):
    g, p = lax.axis_index("grp"), lax.axis_index("pq")
    x, core = g // 2, g % 2
    y, z = p // SIDE, p % SIDE
    slots = blocks.shape[1]
    nblk = SIDE * FAR
    first, second = (y, z), (z, y)
    strides = ((SIDE, 1), (1, SIDE))
    partner = (g + 1 - 2 * core, p)

    def at(order, to_first, to_second):
        return (g, to_first % SIDE * strides[order][0] + to_second % SIDE * strides[order][1])

    barrier = pltpu.get_barrier_semaphore()
    peers = [partner] + [((g + 2 * j) % 8, p) for j in range(1, 4)]
    peers += [at(order, first[order] + d, second[order]) for order in range(2) for d in range(1, SIDE)]
    for device in peers:
        pl.semaphore_signal(barrier, inc=1, device_id=device, device_id_type=MESH)
    load_coef = pltpu.make_async_copy(coef_hbm, own, in_sem.at[0])
    load_blocks = pltpu.make_async_copy(blocks_hbm, blocks, in_sem.at[1])
    load_coef.start()
    load_blocks.start()
    load_coef.wait()
    mine[...] = jnp.concatenate([own[...], own[...]], axis=1)
    pl.semaphore_wait(barrier, len(peers))

    @pl.when(core == 0)
    def _():
        hand = remote(mine, theirs, o_send, o_recv, partner)
        hand.start()
        hand.wait_send()
        remote(coef, coef, d_send, d_recv, partner).wait_recv()

    @pl.when(core == 1)
    def _():
        remote(theirs, theirs, o_send, o_recv, partner).wait_recv()
        low = lax.broadcasted_iota(jnp.int32, (64, TILE), 1) < TILE // 2
        both = jnp.where(low, theirs[...], mine[...])
        for order in range(2):
            coef[order, second[order], 0, x] = both[32 * order : 32 * order + 32]
        for j in range(1, 4):
            for order in range(2):
                piece = coef.at[order, second[order], 0, x]
                remote(piece, piece, x_send, x_recv, ((g + 2 * j) % 8, p)).start()
        six = coef.at[0, 0, pl.ds(0, 3), pl.ds(0, 2)]
        remote(six, six, x_send, x_recv, partner).wait_recv()

        straight = {}
        for d in FAR_FIRST[:-1]:
            for order in range(2):
                place = NEAR_FIRST.index(SIDE - d)
                copy = remote(
                    coef.at[order, second[order], 0],
                    coef.at[order, second[order], place],
                    a_send.at[order],
                    a_recv.at[order, place],
                    at(order, first[order] + d, second[order]),
                )
                copy.start()
                straight[order, place] = copy

        flights, held = {}, {}

        def send_on(order, way, place, step):
            away = step if way == 1 else SIDE - step
            row = (second[order] + away) % SIDE
            if step < hops_of(way, place):
                piece = coef.at[order, row, place]
                to = at(order, first[order], second[order] + (1 if way == 0 else 7))
                copy = remote(piece, piece, b_send.at[order], b_recv.at[order, way, place, step], to)
                copy.start()
                flights[order, way, place, step + 1] = copy
            if step > 0 or way == 0:
                pair = held.setdefault((order, away % SIDE, place // 2), set())
                pair.add(place)
                if len(pair) == 2:
                    piece = coef.at[order, row, pl.ds(place // 2 * 2, 2)]
                    remote(piece, piece, d_send, d_recv, partner).start()

        for step in range(FAR + 1):
            for place in range(SIDE):
                for order in range(2):
                    if step == 0 and place > 0:
                        straight[order, place].wait_recv()
                    for way in range(2):
                        if step <= hops_of(way, place):
                            if step > 0:
                                flights[order, way, place, step].wait_recv()
                            send_on(order, way, place, step)
        remote(six, six, x_send, x_recv, partner).wait_send()
        for order in range(2):
            seven = coef.at[0, 0, pl.ds(0, 7)]
            remote(seven, seven, a_send.at[order], d_recv, partner).wait_send()
            seven = coef.at[0, pl.ds(0, 7)]
            remote(seven, seven, b_send.at[order], d_recv, partner).wait_send()
        remote(coef, coef, d_send, d_recv, partner).wait_send()

    load_blocks.wait()

    def rows_of(tile):
        pieces = []
        for e in range(2):
            y_of, z_of = tile // 4, 2 * (tile % 4) + e
            pieces.append(coef[0, z_of, near_place(y_of - y)])
            pieces.append(coef[1, y_of, near_place(z_of - z)])
        return [jnp.concatenate([piece[n] for piece in pieces], axis=0) for n in range(4)]

    def transform(panel):
        def one_slot(slot, carry):
            ident = list_ref[panel, slot]
            live = slot < count_ref[0, panel]
            which = ident // (nblk * nblk)
            here = pl.ds(pl.multiple_of(slot * TILE, TILE), TILE)
            cols = jnp.concatenate(rows_of(ident % nblk), axis=1)
            half[here, :] = jnp.dot(blocks[panel, slot], cols, preferred_element_type=jnp.float32).astype(BF16)
            rows = rows_of(ident // nblk % nblk)
            keep = [(live & (which == kl)).astype(jnp.float32).astype(BF16) for kl in range(KL)]
            for n in range(4):
                turned = rows[n].T
                for kl in range(KL):
                    left[n, pl.ds(kl * TILE, TILE), here] = turned * keep[kl]
            return carry

        lax.fori_loop(0, slots, one_slot, 0, unroll=UNROLL)
        for m in range(4):
            block = jnp.dot(left[m], half[...], preferred_element_type=jnp.float32)
            block = block.reshape(KL, 2, SIDE, 8, block.shape[1])
            block = jnp.concatenate([block[0], block[1]], axis=2).astype(BF16)
            width = block.shape[3] // 2
            for n in range(2):
                for i in range(SIDE):
                    sums[0, 2 * m + n, panel, far_place(i - z)] = block[n, i, :, :width]
                    sums[1, i, panel, far_place(2 * m + n - y)] = block[n, i, :, width:]

    numbers = {}
    for order in range(2):
        for panel in range(2):
            for part in range(PARTS):
                for way in range(2):
                    for step in range(hops_of(way, part)):
                        numbers[order, panel, way, part, step] = len(numbers)
    hopping = {}

    def hop(order, panel, way, part, step):
        away = hops_of(way, part) - step
        dest = (first[order] + (away if way == 0 else SIDE - away)) % SIDE
        piece = sums.at[order, dest, panel, pl.ds(ROWS * part, ROWS)]
        if step > 0:
            sofar = came.at[numbers[order, panel, way, part, step - 1]]
            sofar[...] = (piece[...].astype(jnp.float32) + sofar[...].astype(jnp.float32)).astype(BF16)
            piece = sofar
        n = numbers[order, panel, way, part, step]
        to = at(order, first[order] + (1 if way == 0 else 7), second[order])
        copy = remote(piece, came.at[n], r_send, r_recv.at[n], to)
        copy.start()
        hopping[order, panel, way, part, step + 1] = copy

    def finish(order, panel, part):
        rows = pl.ds(ROWS * part, ROWS)
        whole = sums[order, first[order], panel, rows].astype(jnp.float32)
        for way in range(2):
            whole = whole + came[numbers[order, panel, way, part, hops_of(way, part) - 1]].astype(jnp.float32)
        total[order, panel, rows] = whole.astype(BF16)
        for i in range(ROWS * part, ROWS * part + ROWS):
            if FAR_FIRST[i]:
                to = at(order, first[order], second[order] + FAR_FIRST[i])
                remote(total.at[order, panel, i], final.at[order, panel, i], s_send, s_recv.at[order, panel], to).start()

    for panel in range(2):
        transform(panel)
        for part in range(PARTS):
            for order in range(2):
                for way in range(2):
                    hop(order, panel, way, part, 0)
    for step in range(1, FAR + 1):
        for panel in range(2):
            for part in range(PARTS):
                for order in range(2):
                    for way in range(2):
                        if step <= hops_of(way, part):
                            hopping[order, panel, way, part, step].wait_recv()
                        if step < hops_of(way, part):
                            hop(order, panel, way, part, step)
                    if step == FAR:
                        finish(order, panel, part)
    for panel in range(2):
        for order in range(2):
            seven = final.at[order, panel, pl.ds(0, 7)]
            remote(seven, seven, s_send, s_recv.at[order, panel], partner).wait_recv()
            rows = total[order, panel, SIDE - 1].astype(jnp.float32)
            for i in range(SIDE - 1):
                rows = rows + final[order, panel, i].astype(jnp.float32)
            width = rows.shape[1]
            for kl in range(KL):
                out_ref[KL * panel + kl, :, pl.ds(width * order, width)] = rows[8 * kl : 8 * kl + 8]

    remote(came, came, r_send, d_recv, partner).wait_send()
    seven = final.at[:, :, pl.ds(0, 7)]
    remote(seven, seven, s_send, d_recv, partner).wait_send()


def body(pair_blocks, block_list, block_count, coef):
    panels, slots = pair_blocks.shape[:2]
    nmo = 4 * TILE
    dma = pltpu.SemaphoreType.DMA
    flights = 2 * panels * PARTS * (2 * FAR - 1)
    return pl.pallas_call(
        kernel,
        name="transform",
        out_shape=jax.ShapeDtypeStruct((panels * KL, 8, nmo), jnp.float32),
        in_specs=[
            pl.BlockSpec(memory_space=pltpu.SMEM),
            pl.BlockSpec(memory_space=pltpu.SMEM),
            pl.BlockSpec(memory_space=pl.ANY),
            pl.BlockSpec(memory_space=pl.ANY),
        ],
        out_specs=pl.BlockSpec(memory_space=pltpu.VMEM),
        scratch_shapes=[
            pltpu.VMEM(coef.shape, BF16),
            pltpu.VMEM((64, TILE), BF16),
            pltpu.VMEM((64, TILE), BF16),
            pltpu.VMEM((2, SIDE, SIDE, 4, 32, TILE), BF16),
            pltpu.VMEM(pair_blocks.shape, BF16),
            pltpu.VMEM((slots * TILE, nmo), BF16),
            pltpu.VMEM((4, KL * TILE, slots * TILE), BF16),
            pltpu.VMEM((2, SIDE, panels, SIDE, KL * 8, nmo // 2), BF16),
            pltpu.VMEM((flights, ROWS, KL * 8, nmo // 2), BF16),
            pltpu.VMEM((2, panels, SIDE, KL * 8, nmo // 2), BF16),
            pltpu.VMEM((2, panels, SIDE, KL * 8, nmo // 2), BF16),
            dma((2,)),
            dma,
            dma,
            dma,
            dma,
            dma((2,)),
            dma((2, SIDE)),
            dma((2,)),
            dma((2, 2, SIDE, FAR)),
            dma,
            dma,
            dma,
            dma((flights,)),
            dma,
            dma((2, 2)),
        ],
        compiler_params=pltpu.CompilerParams(collective_id=0, has_side_effects=True),
    )(block_list, block_count.reshape(1, panels), pair_blocks, coef)


def solution(mesh):
    in_specs = (P("grp", "pq", None, None), P("grp", "pq"), P("grp", "pq"), P("pq", "grp"))
    out_specs = P("grp", "pq", None)
    return jax.shard_map(body, mesh=mesh, in_specs=in_specs, out_specs=out_specs, check_vma=False)
```

time: 75.8 us -> 70.4 us (0.929)
  the two profiles are of different devices: /device:TPU:1 before, /device:TPU:8 now
where the time goes in v3:
time: 70.4 us; the launch traced here: 70.2 us
  Pallas kernels  68.7 us (98%)
  local copies, waits for them, and re-layouts  1.47 us (2%)
    pallas_call x1, Pallas kernels, body(): pl.pallas_call(kernel, name='transform', out_shape=jax.ShapeDtypeStruct((...  68.7 us
    unnamed x1, local copies, waits for them, and re-layouts  1.47 us

profile of v3, /device:TPU:8, one launch (start us, length us, event | category | flops | bytes accessed | tf_op | source)
XLA Modules:
  0.0 70.2 jit_solution(973119645910362669)
XLA Ops:
  0.0 68.7 %transform.1 = f32[4,8,512]{2,1,0:T(8,128)} custom-call(s32[2,18]{1,0:T(2,128)} %list_ref.1, s32[1,2]{1,0:T(1,128)} %bitcast.1, bf16[2,18,128,128]{3,2,1,0:T(8,128)(2,1)} %blocks_hbm.1, bf16[64,64]{1,0:T(8,128)(2,1)} %coef_hbm.1), custom_call_target="tpu_custom_call" | custom-call | tf_op jit(solution)/shard_map/transform/pallas_call | solution.py:251
  68.7 1.5 %copy.6 = f32[4,8,512]{2,1,0:T(8,128)} copy(f32[4,8,512]{2,1,0:T(8,128)} %transform.1) | data formatting | bytes 131072

commit v4 on v3

--- a/solution.py
+++ b/solution.py
@@ -16,11 +16,7 @@
 PARTS = 4
 ROWS = SIDE // PARTS
 UNROLL = 6
-
-
-def near_place(k):
-    n = (k + 2 * SIDE - 1) % SIDE
-    return 2 * n + 1 + (n // FAR) * (13 - 4 * n)
+EARLY = ((0,), (1,), (2,), (3,))
 
 
 def far_place(k):
@@ -81,45 +77,36 @@
         low = lax.broadcasted_iota(jnp.int32, (64, TILE), 1) < TILE // 2
         both = jnp.where(low, theirs[...], mine[...])
         for order in range(2):
-            coef[order, second[order], 0, x] = both[32 * order : 32 * order + 32]
+            coef[order, second[order] * SIDE + first[order], x] = both[32 * order : 32 * order + 32]
         for j in range(1, 4):
             for order in range(2):
-                piece = coef.at[order, second[order], 0, x]
+                piece = coef.at[order, second[order] * SIDE + first[order], x]
                 remote(piece, piece, x_send, x_recv, ((g + 2 * j) % 8, p)).start()
-        six = coef.at[0, 0, pl.ds(0, 3), pl.ds(0, 2)]
+        six = coef.at[0, pl.ds(0, 3), pl.ds(0, 2)]
         remote(six, six, x_send, x_recv, partner).wait_recv()
 
         straight = {}
         for d in FAR_FIRST[:-1]:
             for order in range(2):
                 place = NEAR_FIRST.index(SIDE - d)
-                copy = remote(
-                    coef.at[order, second[order], 0],
-                    coef.at[order, second[order], place],
-                    a_send.at[order],
-                    a_recv.at[order, place],
-                    at(order, first[order] + d, second[order]),
-                )
+                piece = coef.at[order, second[order] * SIDE + first[order]]
+                to = at(order, first[order] + d, second[order])
+                copy = remote(piece, piece, a_send.at[order], a_recv.at[order, place], to)
                 copy.start()
                 straight[order, place] = copy
 
-        flights, held = {}, {}
+        flights = {}
 
         def send_on(order, way, place, step):
-            away = step if way == 1 else SIDE - step
-            row = (second[order] + away) % SIDE
+            row = (second[order] + (step if way == 1 else SIDE - step)) % SIDE
+            piece = coef.at[order, row * SIDE + (first[order] + NEAR_FIRST[place]) % SIDE]
             if step < hops_of(way, place):
-                piece = coef.at[order, row, place]
                 to = at(order, first[order], second[order] + (1 if way == 0 else 7))
                 copy = remote(piece, piece, b_send.at[order], b_recv.at[order, way, place, step], to)
                 copy.start()
                 flights[order, way, place, step + 1] = copy
             if step > 0 or way == 0:
-                pair = held.setdefault((order, away % SIDE, place // 2), set())
-                pair.add(place)
-                if len(pair) == 2:
-                    piece = coef.at[order, row, pl.ds(place // 2 * 2, 2)]
-                    remote(piece, piece, d_send, d_recv, partner).start()
+                remote(piece, piece, d_send, d_recv, partner).start()
 
         for step in range(FAR + 1):
             for place in range(SIDE):
@@ -133,9 +120,9 @@
                             send_on(order, way, place, step)
         remote(six, six, x_send, x_recv, partner).wait_send()
         for order in range(2):
-            seven = coef.at[0, 0, pl.ds(0, 7)]
+            seven = coef.at[0, pl.ds(0, 7)]
             remote(seven, seven, a_send.at[order], d_recv, partner).wait_send()
-            seven = coef.at[0, pl.ds(0, 7)]
+            seven = coef.at[0, pl.ds(0, 7 * SIDE)]
             remote(seven, seven, b_send.at[order], d_recv, partner).wait_send()
         remote(coef, coef, d_send, d_recv, partner).wait_send()
 
@@ -144,12 +131,11 @@
     def rows_of(tile):
         pieces = []
         for e in range(2):
-            y_of, z_of = tile // 4, 2 * (tile % 4) + e
-            pieces.append(coef[0, z_of, near_place(y_of - y)])
-            pieces.append(coef[1, y_of, near_place(z_of - z)])
+            pieces.append(coef[0, (2 * (tile % 4) + e) * SIDE + tile // 4])
+            pieces.append(coef[1, 2 * tile + e])
         return [jnp.concatenate([piece[n] for piece in pieces], axis=0) for n in range(4)]
 
-    def transform(panel):
+    def halves(panel):
         def one_slot(slot, carry):
             ident = list_ref[panel, slot]
             live = slot < count_ref[0, panel]
@@ -162,19 +148,24 @@
             for n in range(4):
                 turned = rows[n].T
                 for kl in range(KL):
-                    left[n, pl.ds(kl * TILE, TILE), here] = turned * keep[kl]
+                    kept = turned * keep[kl]
+                    for i in range(2):
+                        left[2 * n + i, pl.ds(kl * 64, 64), here] = kept[64 * i : 64 * i + 64]
             return carry
 
         lax.fori_loop(0, slots, one_slot, 0, unroll=UNROLL)
-        for m in range(4):
-            block = jnp.dot(left[m], half[...], preferred_element_type=jnp.float32)
-            block = block.reshape(KL, 2, SIDE, 8, block.shape[1])
-            block = jnp.concatenate([block[0], block[1]], axis=2).astype(BF16)
-            width = block.shape[3] // 2
-            for n in range(2):
-                for i in range(SIDE):
-                    sums[0, 2 * m + n, panel, far_place(i - z)] = block[n, i, :, :width]
-                    sums[1, i, panel, far_place(2 * m + n - y)] = block[n, i, :, width:]
+
+    def products(panel, part):
+        y_to = [(y + d) % SIDE for d in FAR_FIRST[2 * part : 2 * part + 2]]
+        lefts = jnp.concatenate([left[y_to[0]], left[y_to[1]]], axis=0)
+        block = jnp.dot(lefts, half[...], preferred_element_type=jnp.float32)
+        block = block.reshape(2, KL, SIDE, 8, block.shape[1])
+        width = block.shape[4] // 2
+        for n in range(2):
+            rows = jnp.concatenate([block[n, 0], block[n, 1]], axis=1).astype(BF16)
+            for i in range(SIDE):
+                sums[0, y_to[n], panel, far_place(i - z)] = rows[i, :, :width]
+                sums[1, i, panel, 2 * part + n] = rows[i, :, width:]
 
     numbers = {}
     for order in range(2):
@@ -210,23 +201,40 @@
                 to = at(order, first[order], second[order] + FAR_FIRST[i])
                 remote(total.at[order, panel, i], final.at[order, panel, i], s_send, s_recv.at[order, panel], to).start()
 
-    for panel in range(2):
-        transform(panel)
-        for part in range(PARTS):
-            for order in range(2):
+    def arrive(step, panel, order, parts):
+        for part in parts:
+            for way in range(2):
+                if step <= hops_of(way, part):
+                    hopping[order, panel, way, part, step].wait_recv()
+                if step < hops_of(way, part):
+                    hop(order, panel, way, part, step)
+            if step == FAR:
+                finish(order, panel, part)
+
+    def leave(panel, part):
+        products(panel, part)
+        if part < 2:
+            for n in range(PARTS):
                 for way in range(2):
-                    hop(order, panel, way, part, 0)
+                    if (way == 1 and hops_of(way, n) < FAR) == (part == 1):
+                        hop(0, panel, way, n, 0)
+        for way in range(2):
+            hop(1, panel, way, part, 0)
+
+    halves(0)
+    for part in range(PARTS):
+        leave(0, part)
+    halves(1)
+    arrive(1, 0, 0, range(PARTS))
+    for part in range(PARTS):
+        arrive(1, 0, 1, EARLY[part])
+        leave(1, part)
     for step in range(1, FAR + 1):
-        for panel in range(2):
-            for part in range(PARTS):
-                for order in range(2):
-                    for way in range(2):
-                        if step <= hops_of(way, part):
-                            hopping[order, panel, way, part, step].wait_recv()
-                        if step < hops_of(way, part):
-                            hop(order, panel, way, part, step)
-                    if step == FAR:
-                        finish(order, panel, part)
+        for order in range(2):
+            if step < FAR:
+                arrive(step + 1, 0, order, range(PARTS))
+        for order in range(2):
+            arrive(step, 1, order, range(PARTS))
     for panel in range(2):
         for order in range(2):
             seven = final.at[order, panel, pl.ds(0, 7)]
@@ -263,10 +271,10 @@
             pltpu.VMEM(coef.shape, BF16),
             pltpu.VMEM((64, TILE), BF16),
             pltpu.VMEM((64, TILE), BF16),
-            pltpu.VMEM((2, SIDE, SIDE, 4, 32, TILE), BF16),
+            pltpu.VMEM((2, SIDE * SIDE, 4, 32, TILE), BF16),
             pltpu.VMEM(pair_blocks.shape, BF16),
             pltpu.VMEM((slots * TILE, nmo), BF16),
-            pltpu.VMEM((4, KL * TILE, slots * TILE), BF16),
+            pltpu.VMEM((SIDE, KL * TILE // 2, slots * TILE), BF16),
             pltpu.VMEM((2, SIDE, panels, SIDE, KL * 8, nmo // 2), BF16),
             pltpu.VMEM((flights, ROWS, KL * 8, nmo // 2), BF16),
             pltpu.VMEM((2, panels, SIDE, KL * 8, nmo // 2), BF16),

time: 70.4 us -> 70.2 us (level)
  no operation moved by 1% of the time
where the time goes in v4:
time: 70.2 us; the launch traced here: 70 us
  Pallas kernels  68.5 us (98%)
  local copies, waits for them, and re-layouts  1.47 us (2%)
    pallas_call x1, Pallas kernels, body(): pl.pallas_call(kernel, name='transform', out_shape=jax.ShapeDtypeStruct((...  68.5 us
    unnamed x1, local copies, waits for them, and re-layouts  1.47 us

profile of v4, /device:TPU:8, one launch (start us, length us, event | category | flops | bytes accessed | tf_op | source)
XLA Modules:
  0.0 70.0 jit_solution(17593312791508115516)
XLA Ops:
  0.0 68.5 %transform.1 = f32[4,8,512]{2,1,0:T(8,128)} custom-call(s32[2,18]{1,0:T(2,128)} %list_ref.1, s32[1,2]{1,0:T(1,128)} %bitcast.1, bf16[2,18,128,128]{3,2,1,0:T(8,128)(2,1)} %blocks_hbm.1, bf16[64,64]{1,0:T(8,128)(2,1)} %coef_hbm.1), custom_call_target="tpu_custom_call" | custom-call | tf_op jit(solution)/shard_map/transform/pallas_call | solution.py:259
  68.5 1.5 %copy.6 = f32[4,8,512]{2,1,0:T(8,128)} copy(f32[4,8,512]{2,1,0:T(8,128)} %transform.1) | data formatting | bytes 131072

commit v5 on v4

--- a/solution.py
+++ b/solution.py
@@ -16,7 +16,13 @@
 PARTS = 4
 ROWS = SIDE // PARTS
 UNROLL = 6
-EARLY = ((0,), (1,), (2,), (3,))
+TWO_STAGES = (False, True)
+ALL = range(PARTS)
+EARLY = ((), ((1, 0, 0, ALL), (1, 0, 1, (0,))), ((1, 0, 1, (1, 2)),), ((1, 0, 1, (3,)),))
+LATE = (
+    (2, 0, 0), (2, 0, 1), (1, 1, 0), (1, 1, 1), (3, 0, 0), (3, 0, 1),
+    (2, 1, 0), (2, 1, 1), (4, 0, 0), (4, 0, 1),
+)
 
 
 def far_place(k):
@@ -35,8 +41,8 @@
 
 
 def kernel(
-    list_ref, count_ref, blocks_hbm, coef_hbm, out_ref,
-    own, mine, theirs, coef, blocks, half, left, sums, came, total, final,
+    list_hbm, count_hbm, blocks_hbm, coef_hbm, out_ref,
+    list_ref, count_ref, own, mine, theirs, coef, blocks, half, left, sums, came, total, final,
     in_sem, o_send, o_recv, x_send, x_recv, a_send, a_recv, b_send, b_recv, d_send, d_recv, r_send, r_recv, s_send, s_recv,
 ):
     g, p = lax.axis_index("grp"), lax.axis_index("pq")
@@ -58,7 +64,11 @@
         pl.semaphore_signal(barrier, inc=1, device_id=device, device_id_type=MESH)
     load_coef = pltpu.make_async_copy(coef_hbm, own, in_sem.at[0])
     load_blocks = pltpu.make_async_copy(blocks_hbm, blocks, in_sem.at[1])
+    load_list = pltpu.make_async_copy(list_hbm, list_ref, in_sem.at[2])
+    load_count = pltpu.make_async_copy(count_hbm, count_ref, in_sem.at[3])
     load_coef.start()
+    load_list.start()
+    load_count.start()
     load_blocks.start()
     load_coef.wait()
     mine[...] = jnp.concatenate([own[...], own[...]], axis=1)
@@ -86,7 +96,7 @@
         remote(six, six, x_send, x_recv, partner).wait_recv()
 
         straight = {}
-        for d in FAR_FIRST[:-1]:
+        for d in NEAR_FIRST[1:]:
             for order in range(2):
                 place = NEAR_FIRST.index(SIDE - d)
                 piece = coef.at[order, second[order] * SIDE + first[order]]
@@ -126,6 +136,8 @@
             remote(seven, seven, b_send.at[order], d_recv, partner).wait_send()
         remote(coef, coef, d_send, d_recv, partner).wait_send()
 
+    load_list.wait()
+    load_count.wait()
     load_blocks.wait()
 
     def rows_of(tile):
@@ -167,74 +179,93 @@
                 sums[0, y_to[n], panel, far_place(i - z)] = rows[i, :, :width]
                 sums[1, i, panel, 2 * part + n] = rows[i, :, width:]
 
-    numbers = {}
+    numbers, hopping = {}, {}
     for order in range(2):
         for panel in range(2):
             for part in range(PARTS):
                 for way in range(2):
-                    for step in range(hops_of(way, part)):
+                    steps = range(hops_of(way, part))
+                    if TWO_STAGES[panel]:
+                        steps = ("over", "one", "two") + (("top",) if hops_of(way, part) == FAR else ())
+                    for step in steps:
                         numbers[order, panel, way, part, step] = len(numbers)
-    hopping = {}
-
-    def hop(order, panel, way, part, step):
-        away = hops_of(way, part) - step
+
+    def send_sum(key, piece, hops):
+        order, _, way, _, _ = key
+        to = at(order, first[order] + (hops if way == 0 else SIDE - hops), second[order])
+        copy = remote(piece, came.at[numbers[key]], r_send, r_recv.at[numbers[key]], to)
+        copy.start()
+        hopping[key] = copy
+
+    def sum_for(order, panel, way, part, away):
         dest = (first[order] + (away if way == 0 else SIDE - away)) % SIDE
-        piece = sums.at[order, dest, panel, pl.ds(ROWS * part, ROWS)]
-        if step > 0:
-            sofar = came.at[numbers[order, panel, way, part, step - 1]]
-            sofar[...] = (piece[...].astype(jnp.float32) + sofar[...].astype(jnp.float32)).astype(BF16)
-            piece = sofar
-        n = numbers[order, panel, way, part, step]
-        to = at(order, first[order] + (1 if way == 0 else 7), second[order])
-        copy = remote(piece, came.at[n], r_send, r_recv.at[n], to)
-        copy.start()
-        hopping[order, panel, way, part, step + 1] = copy
+        return sums.at[order, dest, panel, pl.ds(ROWS * part, ROWS)]
+
+    def added(key, away):
+        hopping[key].wait_recv()
+        sofar = came.at[numbers[key]]
+        piece = sum_for(*key[:4], away)
+        sofar[...] = (piece[...].astype(jnp.float32) + sofar[...].astype(jnp.float32)).astype(BF16)
+        return sofar
 
     def finish(order, panel, part):
         rows = pl.ds(ROWS * part, ROWS)
         whole = sums[order, first[order], panel, rows].astype(jnp.float32)
         for way in range(2):
-            whole = whole + came[numbers[order, panel, way, part, hops_of(way, part) - 1]].astype(jnp.float32)
+            for step in ("one", "two") if TWO_STAGES[panel] else (hops_of(way, part) - 1,):
+                key = (order, panel, way, part, step)
+                hopping[key].wait_recv()
+                whole = whole + came[numbers[key]].astype(jnp.float32)
         total[order, panel, rows] = whole.astype(BF16)
         for i in range(ROWS * part, ROWS * part + ROWS):
             if FAR_FIRST[i]:
                 to = at(order, first[order], second[order] + FAR_FIRST[i])
                 remote(total.at[order, panel, i], final.at[order, panel, i], s_send, s_recv.at[order, panel], to).start()
 
-    def arrive(step, panel, order, parts):
+    def arrive(step, panel, order, parts=range(PARTS)):
+        last = 2 if TWO_STAGES[panel] else FAR
         for part in parts:
             for way in range(2):
-                if step <= hops_of(way, part):
-                    hopping[order, panel, way, part, step].wait_recv()
-                if step < hops_of(way, part):
-                    hop(order, panel, way, part, step)
-            if step == FAR:
+                key = (order, panel, way, part)
+                hops = hops_of(way, part)
+                if TWO_STAGES[panel]:
+                    if step == 1:
+                        send_sum((*key, "one"), added((*key, "over"), 1), 1)
+                        if hops == FAR:
+                            send_sum((*key, "two"), added((*key, "top"), 2), 2)
+                elif step < hops:
+                    send_sum((*key, step), added((*key, step - 1), hops - step), 1)
+            if step == last:
                 finish(order, panel, part)
+
+    def begin(order, panel, part, aways):
+        for way in range(2):
+            key = (order, panel, way, part)
+            hops = hops_of(way, part)
+            if TWO_STAGES[panel]:
+                starts = [("over", 3, 2), ("top", 4, 2) if hops == FAR else ("two", 2, 2)]
+            else:
+                starts = [(0, hops, 1)]
+            for step, away, on in starts:
+                if (away if way == 0 else SIDE - away) in aways:
+                    send_sum((*key, step), sum_for(*key, away), on)
 
     def leave(panel, part):
         products(panel, part)
-        if part < 2:
-            for n in range(PARTS):
-                for way in range(2):
-                    if (way == 1 and hops_of(way, n) < FAR) == (part == 1):
-                        hop(0, panel, way, n, 0)
-        for way in range(2):
-            hop(1, panel, way, part, 0)
+        for n in range(PARTS):
+            begin(0, panel, n, FAR_FIRST[2 * part : 2 * part + 2])
+        begin(1, panel, part, range(SIDE))
 
     halves(0)
     for part in range(PARTS):
         leave(0, part)
     halves(1)
-    arrive(1, 0, 0, range(PARTS))
     for part in range(PARTS):
-        arrive(1, 0, 1, EARLY[part])
+        for step, panel, order, parts in EARLY[part]:
+            arrive(step, panel, order, parts)
         leave(1, part)
-    for step in range(1, FAR + 1):
-        for order in range(2):
-            if step < FAR:
-                arrive(step + 1, 0, order, range(PARTS))
-        for order in range(2):
-            arrive(step, 1, order, range(PARTS))
+    for step, panel, order in LATE:
+        arrive(step, panel, order)
     for panel in range(2):
         for order in range(2):
             seven = final.at[order, panel, pl.ds(0, 7)]
@@ -261,13 +292,15 @@
         name="transform",
         out_shape=jax.ShapeDtypeStruct((panels * KL, 8, nmo), jnp.float32),
         in_specs=[
-            pl.BlockSpec(memory_space=pltpu.SMEM),
-            pl.BlockSpec(memory_space=pltpu.SMEM),
+            pl.BlockSpec(memory_space=pl.ANY),
+            pl.BlockSpec(memory_space=pl.ANY),
             pl.BlockSpec(memory_space=pl.ANY),
             pl.BlockSpec(memory_space=pl.ANY),
         ],
         out_specs=pl.BlockSpec(memory_space=pltpu.VMEM),
         scratch_shapes=[
+            pltpu.SMEM((panels, slots), jnp.int32),
+            pltpu.SMEM((1, panels), jnp.int32),
             pltpu.VMEM(coef.shape, BF16),
             pltpu.VMEM((64, TILE), BF16),
             pltpu.VMEM((64, TILE), BF16),
@@ -279,7 +312,7 @@
             pltpu.VMEM((flights, ROWS, KL * 8, nmo // 2), BF16),
             pltpu.VMEM((2, panels, SIDE, KL * 8, nmo // 2), BF16),
             pltpu.VMEM((2, panels, SIDE, KL * 8, nmo // 2), BF16),
-            dma((2,)),
+            dma((4,)),
             dma,
             dma,
             dma,

time: 70.2 us -> 68.2 us (0.972)
  the two profiles are of different devices: /device:TPU:8 before, /device:TPU:16 now
where the time goes in v5:
time: 68.2 us; the launch traced here: 68 us
  Pallas kernels  66.6 us (98%)
  local copies, waits for them, and re-layouts  1.47 us (2%)
    pallas_call x1, Pallas kernels, body(): pl.pallas_call(kernel, name='transform', out_shape=jax.ShapeDtypeStruct((...  66.6 us
    unnamed x1, local copies, waits for them, and re-layouts  1.47 us

profile of v5, /device:TPU:16, one launch (start us, length us, event | category | flops | bytes accessed | tf_op | source)
XLA Modules:
  0.0 68.0 jit_solution(17739344426001974771)
XLA Ops:
  0.0 66.6 %transform.1 = f32[4,8,512]{2,1,0:T(8,128)} custom-call(s32[2,18]{1,0:T(2,128)} %list_hbm.1, s32[1,2]{1,0:T(1,128)} %bitcast.1, bf16[2,18,128,128]{3,2,1,0:T(8,128)(2,1)} %blocks_hbm.1, bf16[64,64]{1,0:T(8,128)(2,1)} %coef_hbm.1), custom_call_target="tpu_custom_call" | custom-call | tf_op jit(solution)/shard_map/transform/pallas_call | solution.py:290
  66.6 1.5 %copy.6 = f32[4,8,512]{2,1,0:T(8,128)} copy(f32[4,8,512]{2,1,0:T(8,128)} %transform.1) | data formatting | bytes 131072

commit v6 on v5

--- a/solution.py
+++ b/solution.py
@@ -15,7 +15,7 @@
 FAR_FIRST = (4, 3, 5, 2, 6, 1, 7, 0)
 PARTS = 4
 ROWS = SIDE // PARTS
-UNROLL = 6
+UNROLL = 9
 TWO_STAGES = (False, True)
 ALL = range(PARTS)
 EARLY = ((), ((1, 0, 0, ALL), (1, 0, 1, (0,))), ((1, 0, 1, (1, 2)),), ((1, 0, 1, (3,)),))
@@ -42,8 +42,8 @@
 
 def kernel(
     list_hbm, count_hbm, blocks_hbm, coef_hbm, out_ref,
-    list_ref, count_ref, own, mine, theirs, coef, blocks, half, left, sums, came, total, final,
-    in_sem, o_send, o_recv, x_send, x_recv, a_send, a_recv, b_send, b_recv, d_send, d_recv, r_send, r_recv, s_send, s_recv,
+    list_ref, count_ref, own, mine, raw, coef, blocks, half, left, sums, came, total, final,
+    in_sem, o_send, o_recv, a_send, a_recv, b_send, b_recv, d_send, d_recv, r_send, r_recv, s_send, s_recv,
 ):
     g, p = lax.axis_index("grp"), lax.axis_index("pq")
     x, core = g // 2, g % 2
@@ -58,7 +58,7 @@
         return (g, to_first % SIDE * strides[order][0] + to_second % SIDE * strides[order][1])
 
     barrier = pltpu.get_barrier_semaphore()
-    peers = [partner] + [((g + 2 * j) % 8, p) for j in range(1, 4)]
+    peers = [((g + j) % 8, p) for j in range(1, 8)]
     peers += [at(order, first[order] + d, second[order]) for order in range(2) for d in range(1, SIDE)]
     for device in peers:
         pl.semaphore_signal(barrier, inc=1, device_id=device, device_id_type=MESH)
@@ -76,24 +76,22 @@
 
     @pl.when(core == 0)
     def _():
-        hand = remote(mine, theirs, o_send, o_recv, partner)
-        hand.start()
-        hand.wait_send()
+        for j in (1, 3, 5, 7):
+            remote(mine, raw.at[g], o_send, o_recv, ((g + j) % 8, p)).start()
         remote(coef, coef, d_send, d_recv, partner).wait_recv()
 
     @pl.when(core == 1)
     def _():
-        remote(theirs, theirs, o_send, o_recv, partner).wait_recv()
+        for j in (2, 4, 6):
+            remote(mine, raw.at[g], o_send, o_recv, ((g + j) % 8, p)).start()
+        raw[g] = mine[...]
+        seven = raw.at[pl.ds(0, 7)]
+        remote(seven, seven, o_send, o_recv, partner).wait_recv()
         low = lax.broadcasted_iota(jnp.int32, (64, TILE), 1) < TILE // 2
-        both = jnp.where(low, theirs[...], mine[...])
-        for order in range(2):
-            coef[order, second[order] * SIDE + first[order], x] = both[32 * order : 32 * order + 32]
-        for j in range(1, 4):
+        for n in range(4):
+            both = jnp.where(low, raw[2 * n], raw[2 * n + 1])
             for order in range(2):
-                piece = coef.at[order, second[order] * SIDE + first[order], x]
-                remote(piece, piece, x_send, x_recv, ((g + 2 * j) % 8, p)).start()
-        six = coef.at[0, pl.ds(0, 3), pl.ds(0, 2)]
-        remote(six, six, x_send, x_recv, partner).wait_recv()
+                coef[order, second[order] * SIDE + first[order], n] = both[32 * order : 32 * order + 32]
 
         straight = {}
         for d in NEAR_FIRST[1:]:
@@ -128,13 +126,6 @@
                             if step > 0:
                                 flights[order, way, place, step].wait_recv()
                             send_on(order, way, place, step)
-        remote(six, six, x_send, x_recv, partner).wait_send()
-        for order in range(2):
-            seven = coef.at[0, pl.ds(0, 7)]
-            remote(seven, seven, a_send.at[order], d_recv, partner).wait_send()
-            seven = coef.at[0, pl.ds(0, 7 * SIDE)]
-            remote(seven, seven, b_send.at[order], d_recv, partner).wait_send()
-        remote(coef, coef, d_send, d_recv, partner).wait_send()
 
     load_list.wait()
     load_count.wait()
@@ -276,6 +267,22 @@
             width = rows.shape[1]
             for kl in range(KL):
                 out_ref[KL * panel + kl, :, pl.ds(width * order, width)] = rows[8 * kl : 8 * kl + 8]
+
+    @pl.when(core == 0)
+    def _():
+        four = raw.at[pl.ds(0, 4)]
+        remote(four, four, o_send, d_recv, partner).wait_send()
+
+    @pl.when(core == 1)
+    def _():
+        three = raw.at[pl.ds(0, 3)]
+        remote(three, three, o_send, d_recv, partner).wait_send()
+        for order in range(2):
+            seven = coef.at[0, pl.ds(0, 7)]
+            remote(seven, seven, a_send.at[order], d_recv, partner).wait_send()
+            seven = coef.at[0, pl.ds(0, 7 * SIDE)]
+            remote(seven, seven, b_send.at[order], d_recv, partner).wait_send()
+        remote(coef, coef, d_send, d_recv, partner).wait_send()
 
     remote(came, came, r_send, d_recv, partner).wait_send()
     seven = final.at[:, :, pl.ds(0, 7)]
@@ -303,7 +310,7 @@
             pltpu.SMEM((1, panels), jnp.int32),
             pltpu.VMEM(coef.shape, BF16),
             pltpu.VMEM((64, TILE), BF16),
-            pltpu.VMEM((64, TILE), BF16),
+            pltpu.VMEM((8, 64, TILE), BF16),
             pltpu.VMEM((2, SIDE * SIDE, 4, 32, TILE), BF16),
             pltpu.VMEM(pair_blocks.shape, BF16),
             pltpu.VMEM((slots * TILE, nmo), BF16),
@@ -315,8 +322,6 @@
             dma((4,)),
             dma,
             dma,
-            dma,
-            dma,
             dma((2,)),
             dma((2, SIDE)),
             dma((2,)),

time: 68.2 us -> 66.9 us (0.981)
  the two profiles are of different devices: /device:TPU:16 before, /device:TPU:8 now
where the time goes in v6:
time: 66.9 us; the launch traced here: 66.7 us
  Pallas kernels  65.2 us (97%)
  local copies, waits for them, and re-layouts  1.47 us (2%)
    pallas_call x1, Pallas kernels, body(): pl.pallas_call(kernel, name='transform', out_shape=jax.ShapeDtypeStruct((...  65.2 us
    unnamed x1, local copies, waits for them, and re-layouts  1.47 us

profile of v6, /device:TPU:8, one launch (start us, length us, event | category | flops | bytes accessed | tf_op | source)
XLA Modules:
  0.0 66.7 jit_solution(9478518581481532399)
XLA Ops:
  0.0 65.2 %transform.1 = f32[4,8,512]{2,1,0:T(8,128)} custom-call(s32[2,18]{1,0:T(2,128)} %list_hbm.1, s32[1,2]{1,0:T(1,128)} %bitcast.1, bf16[2,18,128,128]{3,2,1,0:T(8,128)(2,1)} %blocks_hbm.1, bf16[64,64]{1,0:T(8,128)(2,1)} %coef_hbm.1), custom_call_target="tpu_custom_call" | custom-call | tf_op jit(solution)/shard_map/transform/pallas_call | solution.py:297
  65.2 1.5 %copy.6 = f32[4,8,512]{2,1,0:T(8,128)} copy(f32[4,8,512]{2,1,0:T(8,128)} %transform.1) | data formatting | bytes 131072

commit v7 on v6

--- a/solution.py
+++ b/solution.py
@@ -18,7 +18,7 @@
 UNROLL = 9
 TWO_STAGES = (False, True)
 ALL = range(PARTS)
-EARLY = ((), ((1, 0, 0, ALL), (1, 0, 1, (0,))), ((1, 0, 1, (1, 2)),), ((1, 0, 1, (3,)),))
+EARLY = (((1, 0, 0, ALL),), ((1, 0, 1, (0, 1)),), ((1, 0, 1, (2,)),), ((1, 0, 1, (3,)),))
 LATE = (
     (2, 0, 0), (2, 0, 1), (1, 1, 0), (1, 1, 1), (3, 0, 0), (3, 0, 1),
     (2, 1, 0), (2, 1, 1), (4, 0, 0), (4, 0, 1),

time: 66.9 us -> 66.8 us (level)
  no operation moved by 1% of the time
where the time goes in v7:
time: 66.8 us; the launch traced here: 66.7 us
  Pallas kernels  65.2 us (98%)
  local copies, waits for them, and re-layouts  1.47 us (2%)
    pallas_call x1, Pallas kernels, body(): pl.pallas_call(kernel, name='transform', out_shape=jax.ShapeDtypeStruct((...  65.2 us
    unnamed x1, local copies, waits for them, and re-layouts  1.47 us

profile of v7, /device:TPU:8, one launch (start us, length us, event | category | flops | bytes accessed | tf_op | source)
XLA Modules:
  0.0 66.7 jit_solution(18217881845996947423)
XLA Ops:
  0.0 65.2 %transform.1 = f32[4,8,512]{2,1,0:T(8,128)} custom-call(s32[2,18]{1,0:T(2,128)} %list_hbm.1, s32[1,2]{1,0:T(1,128)} %bitcast.1, bf16[2,18,128,128]{3,2,1,0:T(8,128)(2,1)} %blocks_hbm.1, bf16[64,64]{1,0:T(8,128)(2,1)} %coef_hbm.1), custom_call_target="tpu_custom_call" | custom-call | tf_op jit(solution)/shard_map/transform/pallas_call | solution.py:297
  65.2 1.5 %copy.6 = f32[4,8,512]{2,1,0:T(8,128)} copy(f32[4,8,512]{2,1,0:T(8,128)} %transform.1) | data formatting | bytes 131072
